TPU v7x, 32 devices: a whole 2x2x4 slice. The times are simulated.
32 devices in a mesh: leaf: 8 (over z, y), grid: 4 (over x, core).
Axes of the slice: x: 2, y: 2, z: 4, core: 2. Of those that a mesh axis runs over, the one named last changes fastest.
Arguments:
- source_leaf: float32 [8, 4096], P(None, ('leaf', 'grid')), may hold values from -6 to 6
- block_leaf: float32 [4096, 128], P(('leaf', 'grid')), may hold values from -0.5 to 0.5
- expand_leaf: float32 [4096, 128], P(('leaf', 'grid')), may hold values from -0.5 to 0.5
- basis_leaf: float32 [4096, 256], P(('leaf', 'grid')), may hold values from -0.25 to 0.25
- pivot_leaf: float32 [4096], P(('leaf', 'grid')), may hold values from -2 to 2
- couple_leaf: float32 [8192, 128], P(('leaf', 'grid')), may hold values from -0.5 to 0.5
- ranks_leaf: int32 [8, 2], replicated, may hold values from 32 to 128
- targets_leaf: int32 [8192], P(('leaf', 'grid')), may hold values from 0 to 2047, as said below
- source_middle: float32 [8, 4096], P(None, ('leaf', 'grid')), may hold values from -6 to 6
- block_middle: float32 [4096, 128], P(('leaf', 'grid')), may hold values from -0.5 to 0.5
- expand_middle: float32 [4096, 128], P(('leaf', 'grid')), may hold values from -0.5 to 0.5
- basis_middle: float32 [4096, 256], P(('leaf', 'grid')), may hold values from -0.1875 to 0.1875
- pivot_middle: float32 [4096], P(('leaf', 'grid')), may hold values from -2 to 2
- couple_middle: float32 [4096, 128], P(('leaf', 'grid')), may hold values from -0.5 to 0.5
- ranks_middle: int32 [4, 2], replicated, may hold values from 32 to 128
- targets_middle: int32 [4096], P(('leaf', 'grid')), may hold values from 0 to 4095, as said below
- source_upper: float32 [8, 4096], P(None, ('leaf', 'grid')), may hold values from -6 to 6
- block_upper: float32 [4096, 128], P(('leaf', 'grid')), may hold values from -0.5 to 0.5
- expand_upper: float32 [4096, 128], P(('leaf', 'grid')), may hold values from -0.5 to 0.5
- basis_upper: float32 [4096, 256], P(('leaf', 'grid')), may hold values from -0.125 to 0.125
- pivot_upper: float32 [4096], P(('leaf', 'grid')), may hold values from -2 to 2
- couple_upper: float32 [4096, 128], P(('leaf', 'grid')), may hold values from -0.5 to 0.5
- ranks_upper: int32 [2, 2], replicated, may hold values from 32 to 128
- targets_upper: int32 [4096], P(('leaf', 'grid')), may hold values from 0 to 4095, as said below
- source_root: float32 [8, 4096], P(None, ('leaf', 'grid')), may hold values from -6 to 6
- block_root: float32 [4096, 128], P(('leaf', 'grid')), may hold values from -0.5 to 0.5
- expand_root: float32 [4096, 128], P(('leaf', 'grid')), may hold values from -0.5 to 0.5
- basis_root: float32 [4096, 256], P(('leaf', 'grid')), may hold values from -0.09375 to 0.09375
- pivot_root: float32 [4096], P(('leaf', 'grid')), may hold values from -2 to 2
- ranks_root: int32 [1, 2], replicated, may hold values from 32 to 128
Outputs:
- answer_leaf: float32 [8, 4096], P(None, ('leaf', 'grid'))
- answer_middle: float32 [8, 4096], P(None, ('leaf', 'grid'))
- answer_upper: float32 [8, 4096], P(None, ('leaf', 'grid'))
- answer_root: float32 [8, 4096], P(None, ('leaf', 'grid'))
Inputs may be any that keep to these rules, and one draw needn't show every extreme that they name: `targets_leaf`: within one leaf front the 1024 entries are distinct; each names a row of the parent front's row vector of 2048 rows. Split that vector's separator part and its update part each evenly, in order, over the parent's devices (leaf then grid); then the rows of one device name at most 32 rows held by any one of them, and exactly that many for some. `targets_middle`: within one middle front the entries are distinct; each names a row of the parent front's row vector of 4096 rows. Split likewise over the parent's devices, the rows of one device name at most 8 rows held by any one of them, and exactly that many for some. `targets_upper`: within one upper front the entries are distinct; each names a row of the root separator. Split evenly in order over all devices, the rows of one device name at most 4 rows held by any one of them, and exactly that many for some.
All inputs are finite; a program needn't handle non-finite values.
Results may differ from a plain program's by a relative error of at most 0.0003.
Values sent between devices are 32-bit elements; how exact they have to be, the bound alone decides.
A program may use at most 128 MiB of HBM per device.

v0:
```python
import jax
import jax.numpy as jnp
from jax import lax
from jax.sharding import PartitionSpec as P

BLOCK = 128
RANK = 128
HIGH_PRECISION = lax.Precision.HIGHEST


def from_partner(value, axis, distance):
    mask = 2**distance
    pairs = [(source, source ^ mask) for source in range(lax.axis_size(axis))]
    return lax.ppermute(value, axis, pairs)


def mult(left, right):
    return jnp.dot(left, right, precision=HIGH_PRECISION, preferred_element_type=jnp.float32)


def inner(left, right):
    return lax.dot_general(
        left,
        right,
        (((0,), (0,)), ((), ())),
        precision=HIGH_PRECISION,
        preferred_element_type=jnp.float32,
    )


def outer(left, right):
    return lax.dot_general(
        left,
        right,
        (((1,), (1,)), ((), ())),
        precision=HIGH_PRECISION,
        preferred_element_type=jnp.float32,
    )


def paired_total(partial_value, bits):
    summed = lax.psum(partial_value, "grid")
    for bit in range(bits):
        summed = summed + from_partner(summed, "leaf", bit)
    return summed


def group_total(partial_value, bits):
    return paired_total(partial_value, bits)


def upper_bit(place, bit):
    return place // (1 << bit) % 2 == 1


def group_extend(stack, bits, place):
    for bit in reversed(range(bits)):
        half = stack.shape[2] // 2
        lower_part = stack[:, :, :half]
        upper_part = stack[:, :, half:]
        flag = upper_bit(place, bit)
        keep = jnp.where(flag, upper_part, lower_part)
        send = jnp.where(flag, lower_part, upper_part)
        stack = keep + from_partner(send, "leaf", bit)
    return lax.psum_scatter(stack, "grid", scatter_dimension=2, tiled=True)


def group_fetch(stack, bits, place):
    current = lax.all_gather(stack, "grid", axis=2, tiled=True)
    for bit in range(bits):
        other = from_partner(current, "leaf", bit)
        flag = upper_bit(place, bit)
        current = jnp.where(
            flag,
            jnp.concatenate([other, current], axis=2),
            jnp.concatenate([current, other], axis=2),
        )
    return current


def forward_level(source, incoming, block, expand, basis, pivot, ranks, bits, front):
    level_batch_index = source if incoming is None else source + incoming
    count, width = level_batch_index.shape
    tiles = block.reshape(width // BLOCK, BLOCK, BLOCK)
    local_portion = jnp.einsum(
        "anh,nhk->ank",
        level_batch_index.reshape(count, width // BLOCK, BLOCK),
        tiles,
        precision=HIGH_PRECISION,
    ).reshape(count, width)
    query_lookup = basis[:, :RANK]
    coupling_right_factor = basis[:, RANK:]
    rank_pair = lax.dynamic_index_in_dim(ranks, front, 0, keepdims=False)
    columns = jnp.arange(RANK, dtype=jnp.int32)
    head_mask_grid = (columns < rank_pair[0]).astype(jnp.float32)
    column_mask_grid = (columns < rank_pair[1]).astype(jnp.float32)
    partial_value = jnp.concatenate(
        [
            mult(level_batch_index, query_lookup),
            mult(local_portion, coupling_right_factor),
            inner(expand, coupling_right_factor),
        ],
        axis=0,
    )
    total = group_total(partial_value, bits)
    hidden_q = total[:count] * head_mask_grid
    cross = total[2 * count :]
    intermediate_entries = local_portion + outer(hidden_q, expand)
    weight_entries = (total[count : 2 * count] + mult(hidden_q, cross)) * column_mask_grid
    return (
        intermediate_entries * pivot[None, :],
        weight_entries,
        (tiles, query_lookup, coupling_right_factor, cross, head_mask_grid, column_mask_grid),
    )


def backward_level(correction_entries, x_upd, couple, expand, parts, bits):
    tiles, query_lookup, coupling_right_factor, cross, head_mask_grid, column_mask_grid = parts
    count, width = correction_entries.shape
    if x_upd is None:
        total = group_total(mult(correction_entries, expand), bits)
        remainder_rows = correction_entries
        right_projection = total * head_mask_grid
    else:
        total = group_total(
            jnp.concatenate([mult(x_upd, couple), mult(correction_entries, expand)], axis=0), bits
        )
        solve_direction = total[:count] * column_mask_grid
        remainder_rows = correction_entries - outer(solve_direction, coupling_right_factor)
        right_projection = (total[count:] - outer(solve_direction, cross)) * head_mask_grid
    local_portion = jnp.einsum(
        "anh,nkh->ank",
        remainder_rows.reshape(count, width // BLOCK, BLOCK),
        tiles,
        precision=HIGH_PRECISION,
    ).reshape(count, width)
    return local_portion + outer(right_projection, query_lookup)


def extend(update, targets, sep_total, has_update, bits, place):
    count = update.shape[0]
    pieces = 2 if has_update else 1
    rows = sep_total * pieces
    buffer = jnp.zeros((count, rows), jnp.float32).at[:, targets].add(update)
    if has_update:
        stack = jnp.stack([buffer[:, :sep_total], buffer[:, sep_total:]])
    else:
        stack = buffer[None]
    return group_extend(stack, bits, place)


def fetch(stack, targets, bits, place):
    front_full = group_fetch(stack, bits, place)
    rows = front_full.transpose(1, 0, 2).reshape(front_full.shape[1], -1)
    return jnp.take(rows, targets, axis=1)


def shards(
    source_leaf,
    block_leaf,
    expand_leaf,
    basis_leaf,
    pivot_leaf,
    couple_leaf,
    ranks_leaf,
    targets_leaf,
    source_middle,
    block_middle,
    expand_middle,
    basis_middle,
    pivot_middle,
    couple_middle,
    ranks_middle,
    targets_middle,
    source_upper,
    block_upper,
    expand_upper,
    basis_upper,
    pivot_upper,
    couple_upper,
    ranks_upper,
    targets_upper,
    source_root,
    block_root,
    expand_root,
    basis_root,
    pivot_root,
    ranks_root,
):
    levels = [
        (
            source_leaf,
            block_leaf,
            expand_leaf,
            basis_leaf,
            pivot_leaf,
            couple_leaf,
            ranks_leaf,
            targets_leaf,
        ),
        (
            source_middle,
            block_middle,
            expand_middle,
            basis_middle,
            pivot_middle,
            couple_middle,
            ranks_middle,
            targets_middle,
        ),
        (
            source_upper,
            block_upper,
            expand_upper,
            basis_upper,
            pivot_upper,
            couple_upper,
            ranks_upper,
            targets_upper,
        ),
        (source_root, block_root, expand_root, basis_root, pivot_root, None, ranks_root, None),
    ]
    leaves = lax.axis_size("leaf")
    across = lax.axis_size("grid")
    place = lax.axis_index("leaf")
    depth = leaves.bit_length() - 1
    groups = [1, leaves // 4, leaves // 2, leaves]
    bit_counts = [0, depth - 2, depth - 1, depth]
    owners = [place // groups[level] for level in range(4)]
    inc_sep = None
    inc_upd = None
    saved = []
    for level in range(4):
        source, block, expand, basis, pivot, couple, ranks, targets = levels[level]
        correction_entries, weight_entries, parts = forward_level(
            source, inc_sep, block, expand, basis, pivot, ranks, bit_counts[level], owners[level]
        )
        saved.append((correction_entries, parts))
        if level < 3:
            update = -outer(weight_entries, couple)
            if inc_upd is not None:
                update = update + inc_upd
            sep_total = levels[level + 1][0].shape[1] * across * groups[level + 1]
            has_update = level + 1 < 3
            stack = extend(update, targets, sep_total, has_update, bit_counts[level + 1], place)
            inc_sep = stack[0]
            inc_upd = stack[1] if has_update else None
    answers = [None, None, None, None]
    parent_stack = None
    for level in (3, 2, 1, 0):
        correction_entries, parts = saved[level]
        couple = levels[level][5]
        expand = levels[level][2]
        targets = levels[level][7]
        x_upd = None
        if level < 3:
            x_upd = fetch(parent_stack, targets, bit_counts[level + 1], place)
        xvals = backward_level(correction_entries, x_upd, couple, expand, parts, bit_counts[level])
        answers[level] = xvals
        if level > 0:
            parent_stack = xvals[None] if x_upd is None else jnp.stack([xvals, x_upd])
    return (answers[0], answers[1], answers[2], answers[3])


def solution(mesh):
    in_specs = (
        P(None, ("leaf", "grid")),
        P(("leaf", "grid"), None),
        P(("leaf", "grid"), None),
        P(("leaf", "grid"), None),
        P(("leaf", "grid")),
        P(("leaf", "grid"), None),
        P(),
        P(("leaf", "grid")),
        P(None, ("leaf", "grid")),
        P(("leaf", "grid"), None),
        P(("leaf", "grid"), None),
        P(("leaf", "grid"), None),
        P(("leaf", "grid")),
        P(("leaf", "grid"), None),
        P(),
        P(("leaf", "grid")),
        P(None, ("leaf", "grid")),
        P(("leaf", "grid"), None),
        P(("leaf", "grid"), None),
        P(("leaf", "grid"), None),
        P(("leaf", "grid")),
        P(("leaf", "grid"), None),
        P(),
        P(("leaf", "grid")),
        P(None, ("leaf", "grid")),
        P(("leaf", "grid"), None),
        P(("leaf", "grid"), None),
        P(("leaf", "grid"), None),
        P(("leaf", "grid")),
        P(),
    )
    out_specs = (
        P(None, ("leaf", "grid")),
        P(None, ("leaf", "grid")),
        P(None, ("leaf", "grid")),
        P(None, ("leaf", "grid")),
    )
    return jax.shard_map(shards, mesh=mesh, in_specs=in_specs, out_specs=out_specs, check_vma=False)
```

profile of v0, /device:TPU:0, one launch (start us, length us, event | category | flops | bytes accessed | tf_op | source)
XLA Modules:
  0.0 397.3 jit_solution(7661426514770940477)
XLA Ops:
  17.3 27.4 %all-reduce.5.cloned.1.call-done = f32[144,128]{1,0:T(8,128)} async-done(((f32[144,128]{1,0:T(8,128)}), f32[144,128]{1,0:T(8,128)}) %all-reduce.5.cloned.1.call-update) | async-done | bytes 73744 | tf_op jit(solution)/shard_map/psum | solution.py:42
  53.4 21.0 %reduce-scatter.4.cloned.1.call-done = f32[2,8,128]{2,1,0:T(8,128)} async-done(((f32[2,8,512]{2,1,0:T(8,128)}), f32[2,8,128]{2,1,0:T(8,128)}) %reduce-scatter.4.cloned.1.call-update) | async-done | bytes 8208 | tf_op jit(solution)/shard_map/reduce_scatter | solution.py:65
  77.7 29.1 %all-reduce.7.cloned.1.call-done = f32[144,128]{1,0:T(8,128)} async-done(((f32[144,128]{1,0:T(8,128)}), f32[144,128]{1,0:T(8,128)}) %all-reduce.7.cloned.1.call-update) | async-done | bytes 73744 | tf_op jit(solution)/shard_map/psum | solution.py:42
  128.0 21.2 %reduce-scatter.6.cloned.1.call-done = f32[2,8,128]{2,1,0:T(8,128)} async-done(((f32[2,8,512]{2,1,0:T(8,128)}), f32[2,8,128]{2,1,0:T(8,128)}) %reduce-scatter.6.cloned.1.call-update) | async-done | bytes 8208 | tf_op jit(solution)/shard_map/reduce_scatter | solution.py:65
  152.4 29.2 %all-reduce.9.cloned.1.call-done = f32[144,128]{1,0:T(8,128)} async-done(((f32[144,128]{1,0:T(8,128)}), f32[144,128]{1,0:T(8,128)}) %all-reduce.9.cloned.1.call-update) | async-done | bytes 73744 | tf_op jit(solution)/shard_map/psum | solution.py:42
  196.0 2.7 collective-permute-start.6
  198.7 2.8 collective-permute-done.6
  205.2 9.0 %collective-permute-done.7 = f32[1,8,1024]{1,2,0:T(8,128)S(1)} collective-permute-done((f32[1,8,1024]{1,2,0:T(8,128)S(1)}, f32[1,8,1024]{1,2,0:T(8,128)S(1)}, u32[]{:S(2)}, u32[]{:S(2)}) %collective-permute-start.7) | collective-permute-done | bytes 32800 | tf_op jit(solution)/shard_map/ppermute | solution.py:14
  216.7 4.2 %collective-permute-done.8 = f32[1,8,512]{1,2,0:T(8,128)S(1)} collective-permute-done((f32[1,8,512]{1,2,0:T(8,128)S(1)}, f32[1,8,512]{1,2,0:T(8,128)S(1)}, u32[]{:S(2)}, u32[]{:S(2)}) %collective-permute-start.8) | collective-permute-done | bytes 16416 | tf_op jit(solution)/shard_map/ppermute | solution.py:14
  222.3 20.4 %reduce-scatter.8.cloned.1.call-done = f32[1,8,128]{1,2,0:T(8,128)} async-done(((f32[1,8,512]{1,2,0:T(8,128)}), f32[1,8,128]{1,2,0:T(8,128)}) %reduce-scatter.8.cloned.1.call-update) | async-done | bytes 4112 | tf_op jit(solution)/shard_map/reduce_scatter | solution.py:65
  246.3 29.2 %all-reduce.11.cloned.1.call-done = f32[144,128]{1,0:T(8,128)} async-done(((f32[144,128]{1,0:T(8,128)}), f32[144,128]{1,0:T(8,128)}) %all-reduce.11.cloned.1.call-update) | async-done | bytes 73744 | tf_op jit(solution)/shard_map/psum | solution.py:42
  277.4 3.0 collective-permute-done.9
  283.1 2.6 collective-permute-done.10
  285.7 2.7 collective-permute-start.11
  288.5 2.5 collective-permute-done.11
  291.4 5.9 %psum.60 = f32[8,128]{1,0:T(8,128)S(1)} all-reduce(f32[8,128]{1,0:T(8,128)S(1)} %fusion.123), channel_id=1, replica_groups=mesh['leaf'=8,'grid'=4] {'grid'}, use_global_device_ids=true, to_apply=%region_10.11 | all-reduce | flops 1024 | bytes 8192 | tf_op jit(solution)/shard_map/psum | solution.py:42
  304.6 3.0 collective-permute-start.14
  309.4 5.6 %all-gather = f32[8,512]{1,0:T(8,128)S(1)} all-gather(f32[8,128]{1,0:T(8,128)S(1)} %convolution_add_fusion.3), channel_id=2, replica_groups=mesh['leaf'=8,'grid'=4] {'grid'}, dimensions={1}, use_global_device_ids=true | all-gather | bytes 20480 | tf_op jit(solution)/shard_map/all_gather | solution.py:69
  322.6 3.0 collective-permute-start.17
  330.0 5.8 %psum.61 = f32[16,128]{1,0:T(8,128)S(1)} all-reduce(f32[16,128]{1,0:T(8,128)S(1)} %pad_maximum_fusion.6), channel_id=1, replica_groups=mesh['leaf'=8,'grid'=4] {'grid'}, use_global_device_ids=true, to_apply=%region_11.13 | all-reduce | flops 2048 | bytes 16384 | tf_op jit(solution)/shard_map/psum | solution.py:42
  346.0 5.5 %all_gather.10 = f32[2,8,512]{2,1,0:T(8,128)S(1)} all-gather(f32[2,8,128]{2,1,0:T(8,128)S(1)} %pad_maximum_fusion.7), channel_id=1, replica_groups=mesh['leaf'=8,'grid'=4] {'grid'}, dimensions={2}, use_global_device_ids=true | all-gather | bytes 40960 | tf_op jit(solution)/shard_map/all_gather | solution.py:69
  361.3 5.8 %psum.62 = f32[16,128]{1,0:T(8,128)S(1)} all-reduce(f32[16,128]{1,0:T(8,128)S(1)} %pad_maximum_fusion.8), channel_id=1, replica_groups=mesh['leaf'=8,'grid'=4] {'grid'}, use_global_device_ids=true, to_apply=%region_12.14 | all-reduce | flops 2048 | bytes 16384 | tf_op jit(solution)/shard_map/psum | solution.py:42
  371.7 5.3 %all_gather.11 = f32[2,8,512]{2,1,0:T(8,128)S(1)} all-gather(f32[2,8,128]{2,1,0:T(8,128)S(1)} %pad_maximum_fusion.9), channel_id=1, replica_groups=mesh['leaf'=8,'grid'=4] {'grid'}, dimensions={2}, use_global_device_ids=true | all-gather | bytes 40960 | tf_op jit(solution)/shard_map/all_gather | solution.py:69
  382.4 6.5 %psum.63 = f32[16,128]{1,0:T(8,128)S(1)} all-reduce(f32[16,128]{1,0:T(8,128)S(1)} %pad_maximum_fusion.10), channel_id=1, replica_groups=mesh['leaf'=8,'grid'=4] {'grid'}, use_global_device_ids=true, to_apply=%region_13.15 | all-reduce | flops 2048 | bytes 16384 | tf_op jit(solution)/shard_map/psum | solution.py:42
  (304 shorter events, 128.9 us)
Async XLA Ops:
  7.2 37.5 %all-reduce.5.cloned.1.call-start = ((), (), s32[]{:S(2)}) async-start(), calls=%async_computation.3 | async-start | bytes 147456 | tf_op jit(solution)/shard_map/psum | solution.py:42
  12.1 62.3 %reduce-scatter.4.cloned.1.call-start = ((), (), s32[]{:S(2)}) async-start(), calls=%async_computation.4 | async-start | bytes 40960 | tf_op jit(solution)/shard_map/reduce_scatter | solution.py:65
  48.2 4.0 collective-permute-start
  52.8 54.0 %all-reduce.7.cloned.1.call-start = ((), (), s32[]{:S(2)}) async-start(), calls=%async_computation.5 | async-start | bytes 147456 | tf_op jit(solution)/shard_map/psum | solution.py:42
  77.0 72.3 %reduce-scatter.6.cloned.1.call-start = ((), (), s32[]{:S(2)}) async-start(), calls=%async_computation.6 | async-start | bytes 40960 | tf_op jit(solution)/shard_map/reduce_scatter | solution.py:65
  106.8 4.9 %collective-permute-start.1 = (f32[144,128]{1,0:T(8,128)}, f32[144,128]{1,0:T(8,128)S(1)}, u32[]{:S(2)}, u32[]{:S(2)}) collective-permute-start(f32[144,128]{1,0:T(8,128)} %all-reduce.7.cloned.1.call-done), channel_id=1, source_target_pairs={{0,4},{4,0},{8,12},{12,8},{16,20},{20,16},{24,28},{28,24},{1,5},{5... | collective-permute-start | bytes 221192 | tf_op jit(solution)/shard_map/ppermute | solution.py:14
  118.9 4.3 %collective-permute-start.2 = (f32[2,8,1024]{2,1,0:T(8,128)S(1)}, f32[2,8,1024]{2,1,0:T(8,128)S(1)}, u32[]{:S(2)}, u32[]{:S(2)}) collective-permute-start(f32[2,8,1024]{2,1,0:T(8,128)S(1)} %broadcast_select_fusion), channel_id=1, source_target_pairs={{0,8},{4,12},{8,0},{12,4},{16,24},{20,28},{24,16},{28,20},{1,9},{5... | collective-permute-start | bytes 196616 | tf_op jit(solution)/shard_map/ppermute | solution.py:14
  123.3 4.0 %collective-permute-start.3 = (f32[2,8,512]{2,1,0:T(8,128)S(1)}, f32[2,8,512]{2,1,0:T(8,128)S(1)}, u32[]{:S(2)}, u32[]{:S(2)}) collective-permute-start(f32[2,8,512]{2,1,0:T(8,128)S(1)} %slice_select_fusion.3), channel_id=1, source_target_pairs={{0,4},{4,0},{8,12},{12,8},{16,20},{20,16},{24,28},{28,24},{1,5},{5... | collective-permute-start | bytes 98312 | tf_op jit(solution)/shard_map/ppermute | solution.py:14
  127.9 53.7 %all-reduce.9.cloned.1.call-start = ((), (), s32[]{:S(2)}) async-start(), calls=%async_computation.7 | async-start | bytes 147456 | tf_op jit(solution)/shard_map/psum | solution.py:42
  151.8 90.8 %reduce-scatter.8.cloned.1.call-start = ((), (), s32[]{:S(2)}) async-start(), calls=%async_computation.8 | async-start | bytes 327680 | tf_op jit(solution)/shard_map/reduce_scatter | solution.py:65
  181.6 4.9 %collective-permute-start.4 = (f32[144,128]{1,0:T(8,128)}, f32[144,128]{1,0:T(8,128)S(1)}, u32[]{:S(2)}, u32[]{:S(2)}) collective-permute-start(f32[144,128]{1,0:T(8,128)} %all-reduce.9.cloned.1.call-done), channel_id=1, source_target_pairs={{0,4},{4,0},{8,12},{12,8},{16,20},{20,16},{24,28},{28,24},{1,5},{5... | collective-permute-start | bytes 221192 | tf_op jit(solution)/shard_map/ppermute | solution.py:14
  187.4 4.4 %collective-permute-start.5 = (f32[144,128]{1,0:T(8,128)S(1)}, f32[144,128]{1,0:T(8,128)S(1)}, u32[]{:S(2)}, u32[]{:S(2)}) collective-permute-start(f32[144,128]{1,0:T(8,128)S(1)} %add.207), channel_id=1, source_target_pairs={{0,8},{4,12},{8,0},{12,4},{16,24},{20,28},{24,16},{28,20},{1,9},{5... | collective-permute-start | bytes 221192 | tf_op jit(solution)/shard_map/ppermute | solution.py:14
  196.0 5.5 %collective-permute-start.6 = (f32[1,8,2048]{2,1,0:T(8,128)}, f32[1,8,2048]{2,1,0:T(8,128)}, u32[]{:S(2)}, u32[]{:S(2)}) collective-permute-start(f32[1,8,2048]{2,1,0:T(8,128)} %copy.65), channel_id=1, source_target_pairs={{0,16},{4,20},{8,24},{12,28},{16,0},{20,4},{24,8},{28,12},{1,17},{... | collective-permute-start | bytes 196616 | tf_op jit(solution)/shard_map/ppermute | solution.py:14
  203.0 11.2 %collective-permute-start.7 = (f32[1,8,1024]{1,2,0:T(8,128)S(1)}, f32[1,8,1024]{1,2,0:T(8,128)S(1)}, u32[]{:S(2)}, u32[]{:S(2)}) collective-permute-start(f32[1,8,1024]{1,2,0:T(8,128)S(1)} %slice_select_fusion.1), channel_id=1, source_target_pairs={{0,8},{4,12},{8,0},{12,4},{16,24},{20,28},{24,16},{28,20},{1,9},{5... | collective-permute-start | bytes 98312 | tf_op jit(solution)/shard_map/ppermute | solution.py:14
  214.4 6.4 %collective-permute-start.8 = (f32[1,8,512]{1,2,0:T(8,128)S(1)}, f32[1,8,512]{1,2,0:T(8,128)S(1)}, u32[]{:S(2)}, u32[]{:S(2)}) collective-permute-start(f32[1,8,512]{1,2,0:T(8,128)S(1)} %slice_select_fusion.2), channel_id=1, source_target_pairs={{0,4},{4,0},{8,12},{12,8},{16,20},{20,16},{24,28},{28,24},{1,5},{5... | collective-permute-start | bytes 49160 | tf_op jit(solution)/shard_map/ppermute | solution.py:14
  221.6 53.9 %all-reduce.11.cloned.1.call-start = ((), (), s32[]{:S(2)}) async-start(), calls=%async_computation.9 | async-start | bytes 147456 | tf_op jit(solution)/shard_map/psum | solution.py:42
  275.5 4.9 %collective-permute-start.9 = (f32[144,128]{1,0:T(8,128)}, f32[144,128]{1,0:T(8,128)S(1)}, u32[]{:S(2)}, u32[]{:S(2)}) collective-permute-start(f32[144,128]{1,0:T(8,128)} %all-reduce.11.cloned.1.call-done), channel_id=1, source_target_pairs={{0,4},{4,0},{8,12},{12,8},{16,20},{20,16},{24,28},{28,24},{1,5},{5... | collective-permute-start | bytes 221192 | tf_op jit(solution)/shard_map/ppermute | solution.py:14
  281.3 4.4 %collective-permute-start.10 = (f32[144,128]{1,0:T(8,128)S(1)}, f32[144,128]{1,0:T(8,128)S(1)}, u32[]{:S(2)}, u32[]{:S(2)}) collective-permute-start(f32[144,128]{1,0:T(8,128)S(1)} %add.219), channel_id=1, source_target_pairs={{0,8},{4,12},{8,0},{12,4},{16,24},{20,28},{24,16},{28,20},{1,9},{5... | collective-permute-start | bytes 221192 | tf_op jit(solution)/shard_map/ppermute | solution.py:14
  285.7 5.3 %collective-permute-start.11 = (f32[144,128]{1,0:T(8,128)S(1)}, f32[144,128]{1,0:T(8,128)S(1)}, u32[]{:S(2)}, u32[]{:S(2)}) collective-permute-start(f32[144,128]{1,0:T(8,128)S(1)} %add.220), channel_id=1, source_target_pairs={{0,16},{4,20},{8,24},{12,28},{16,0},{20,4},{24,8},{28,12},{1,17},{... | collective-permute-start | bytes 221192 | tf_op jit(solution)/shard_map/ppermute | solution.py:14
  304.6 4.6 %collective-permute-start.14 = (f32[8,128]{1,0:T(8,128)S(1)}, f32[8,128]{1,0:T(8,128)S(1)}, u32[]{:S(2)}, u32[]{:S(2)}) collective-permute-start(f32[8,128]{1,0:T(8,128)S(1)} %add.224), channel_id=1, source_target_pairs={{0,16},{4,20},{8,24},{12,28},{16,0},{20,4},{24,8},{28,12},{1,17},{... | collective-permute-start | bytes 12296 | tf_op jit(solution)/shard_map/ppermute | solution.py:14
  318.7 3.9 collective-permute-start.16
  322.6 5.2 %collective-permute-start.17 = (f32[1,8,2048]{2,1,0:T(8,128)S(1)}, f32[1,8,2048]{2,1,0:T(8,128)S(1)}, u32[]{:S(2)}, u32[]{:S(2)}) collective-permute-start(f32[1,8,2048]{2,1,0:T(8,128)S(1)} %maximum_select_fusion.2), channel_id=1, source_target_pairs={{0,16},{4,20},{8,24},{12,28},{16,0},{20,4},{24,8},{28,12},{1,17},{... | collective-permute-start | bytes 196616 | tf_op jit(solution)/shard_map/ppermute | solution.py:14
  351.5 3.9 collective-permute-start.20
  355.4 4.3 %collective-permute-start.21 = (f32[2,8,1024]{2,1,0:T(8,128)S(1)}, f32[2,8,1024]{2,1,0:T(8,128)S(1)}, u32[]{:S(2)}, u32[]{:S(2)}) collective-permute-start(f32[2,8,1024]{2,1,0:T(8,128)S(1)} %maximum_select_fusion.4), channel_id=1, source_target_pairs={{0,8},{4,12},{8,0},{12,4},{16,24},{20,28},{24,16},{28,20},{1,9},{5... | collective-permute-start | bytes 196616 | tf_op jit(solution)/shard_map/ppermute | solution.py:14
  (67 other events, 2687.7 us)
Sparse Core Ops, SparseCore 0:
  12.2 32.3 all-reduce.4
  52.9 21.4 reduce-scatter.3
  77.1 29.6 all-reduce.6
  128.0 21.1 reduce-scatter.5
  151.9 29.6 all-reduce.8
  221.7 20.8 reduce-scatter.7
  245.8 29.6 all-reduce.10
where the time goes:
time: 398 us; the launch traced here: 397 us
  waiting for transfers between devices  239 us (60%)
  starting transfers between devices  45.5 us (11%)
  blocking collectives  40.3 us (10%)
  matrix products  24 us (6%)
  other arithmetic  20.3 us (5%)
  between operations  15.1 us (4%)
  local copies, waits for them, and re-layouts  13.5 us (3%)
    psum x4, waiting for transfers between devices, paired_total(): summed = lax.psum(partial_value, 'grid')  115 us
    reduce_scatter x3, waiting for transfers between devices, group_extend(): return lax.psum_scatter(stack, 'grid', scatter_dimension=2, tiled=True)  62.6 us
    ppermute x24, waiting for transfers between devices, from_partner(): return lax.ppermute(value, axis, pairs)  60.9 us
    ppermute x24, starting transfers between devices, from_partner(): return lax.ppermute(value, axis, pairs)  45.2 us
    psum x4, blocking collectives, paired_total(): summed = lax.psum(partial_value, 'grid')  24 us
    all_gather x3, blocking collectives, group_fetch(): current = lax.all_gather(stack, 'grid', axis=2, tiled=True)  16.4 us
    dot_general x18, matrix products, mult(): jnp.dot(left, right, precision=HIGH_PRECISION, preferred_element_type=jnp...  8.73 us
  transfers between devices with their start and end apart: 31, of which 31 were waited for; matrix products, arithmetic and copies ran while one was open for 3% of the time, Pallas kernels for 0%

commit v1 on v0

--- a/solution.py
+++ b/solution.py
@@ -39,7 +39,10 @@
 
 
 def paired_total(partial_value, bits):
-    summed = lax.psum(partial_value, "grid")
+    count_2, summed = (lax.axis_size("grid"), partial_value)
+    for hop in [1 << k for k in range(count_2.bit_length() - 1)]:
+        pairs_2 = [(i, i ^ hop) for i in range(count_2)]
+        summed = summed + lax.ppermute(summed, "grid", pairs_2)
     for bit in range(bits):
         summed = summed + from_partner(summed, "leaf", bit)
     return summed

time: 398 us -> 284 us (0.71)
  waiting for transfers between devices: 239 us -> 158 us
  blocking collectives: 40.3 us -> 15.8 us
  other arithmetic: 20.3 us -> 12.2 us
  matrix products: 24 us -> 19.9 us
    psum x4 -> x0, waiting for transfers between devices: 115 us -> none  [paired_total(): summed = lax.psum(partial_value, 'grid')]
    ppermute x0 -> x16, waiting for transfers between devices: none -> 33.3 us  [paired_total(): summed = summed + lax.ppermute(summed, 'grid', pairs_2)]
    psum x4 -> x0, blocking collectives: 24 us -> none  [paired_total(): summed = lax.psum(partial_value, 'grid')]
    ppermute x0 -> x16, starting transfers between devices: none -> 6.56 us  [paired_total(): summed = summed + lax.ppermute(summed, 'grid', pairs_2)]
  transfers between devices with their start and end apart: 31 -> 43, of which waited for: 31 -> 42; matrix products, arithmetic and copies ran while one was open for 3% -> 4% of each run, Pallas kernels for 0% -> 0%
where the time goes in v1:
time: 284 us
  waiting for transfers between devices  158 us (56%)
  starting transfers between devices  49 us (17%)
  matrix products  19.9 us (7%)
  blocking collectives  15.8 us (6%)
  between operations  14.9 us (5%)
  local copies, waits for them, and re-layouts  13.9 us (5%)
  other arithmetic  12.2 us (4%)
    ppermute x24, waiting for transfers between devices, from_partner(): return lax.ppermute(value, axis, pairs)  63.5 us
    reduce_scatter x3, waiting for transfers between devices, group_extend(): return lax.psum_scatter(stack, 'grid', scatter_dimension=2, tiled=True)  61 us
    ppermute x24, starting transfers between devices, from_partner(): return lax.ppermute(value, axis, pairs)  42.3 us
    ppermute x16, waiting for transfers between devices, paired_total(): summed = summed + lax.ppermute(summed, 'grid', pairs_2)  33.3 us
    all_gather x3, blocking collectives, group_fetch(): current = lax.all_gather(stack, 'grid', axis=2, tiled=True)  15.8 us
    dot_general x18, matrix products, mult(): jnp.dot(left, right, precision=HIGH_PRECISION, preferred_element_type=jnp...  7.23 us
    ppermute x16, starting transfers between devices, paired_total(): summed = summed + lax.ppermute(summed, 'grid', pairs_2)  6.56 us
  transfers between devices with their start and end apart: 43, of which 42 were waited for; matrix products, arithmetic and copies ran while one was open for 4% of the time, Pallas kernels for 0%

profile of v1, /device:TPU:0, one launch (start us, length us, event | category | flops | bytes accessed | tf_op | source)
XLA Modules:
  0.0 283.6 jit_solution(15736979826174918743)
XLA Ops:
  15.8 2.6 collective-permute-start.1
  29.3 21.0 %reduce-scatter.4.cloned.1.call-done = f32[2,8,128]{2,1,0:T(8,128)} async-done(((f32[2,8,512]{2,1,0:T(8,128)}), f32[2,8,128]{2,1,0:T(8,128)}) %reduce-scatter.4.cloned.1.call-update) | async-done | bytes 8208 | tf_op jit(solution)/shard_map/reduce_scatter | solution.py:68
  54.4 3.5 %collective-permute-done.4 = f32[144,128]{1,0:T(8,128)S(1)} collective-permute-done((f32[144,128]{1,0:T(8,128)S(1)}, f32[144,128]{1,0:T(8,128)S(1)}, u32[]{:S(2)}, u32[]{:S(2)}) %collective-permute-start.4) | collective-permute-done | bytes 73760 | tf_op jit(solution)/shard_map/ppermute | solution.py:45
  70.2 2.8 collective-permute-done.6
  77.8 19.6 %reduce-scatter.6.cloned.1.call-done = f32[2,8,128]{2,1,0:T(8,128)} async-done(((f32[2,8,512]{2,1,0:T(8,128)}), f32[2,8,128]{2,1,0:T(8,128)}) %reduce-scatter.6.cloned.1.call-update) | async-done | bytes 8208 | tf_op jit(solution)/shard_map/reduce_scatter | solution.py:68
  101.4 3.6 %collective-permute-done.9 = f32[144,128]{1,0:T(8,128)S(1)} collective-permute-done((f32[144,128]{1,0:T(8,128)S(1)}, f32[144,128]{1,0:T(8,128)S(1)}, u32[]{:S(2)}, u32[]{:S(2)}) %collective-permute-start.9) | collective-permute-done | bytes 73760 | tf_op jit(solution)/shard_map/ppermute | solution.py:45
  118.1 2.4 collective-permute-start.12
  120.5 3.1 %collective-permute-done.12 = f32[1,8,2048]{2,1,0:T(8,128)} collective-permute-done((f32[1,8,2048]{2,1,0:T(8,128)}, f32[1,8,2048]{2,1,0:T(8,128)}, u32[]{:S(2)}, u32[]{:S(2)}) %collective-permute-start.12) | collective-permute-done | bytes 65568 | tf_op jit(solution)/shard_map/ppermute | solution.py:14
  126.6 8.1 %collective-permute-done.13 = f32[1,8,1024]{1,2,0:T(8,128)S(1)} collective-permute-done((f32[1,8,1024]{1,2,0:T(8,128)S(1)}, f32[1,8,1024]{1,2,0:T(8,128)S(1)}, u32[]{:S(2)}, u32[]{:S(2)}) %collective-permute-start.13) | collective-permute-done | bytes 32800 | tf_op jit(solution)/shard_map/ppermute | solution.py:14
  136.5 4.9 %collective-permute-done.14 = f32[1,8,512]{1,2,0:T(8,128)S(1)} collective-permute-done((f32[1,8,512]{1,2,0:T(8,128)S(1)}, f32[1,8,512]{1,2,0:T(8,128)S(1)}, u32[]{:S(2)}, u32[]{:S(2)}) %collective-permute-start.14) | collective-permute-done | bytes 16416 | tf_op jit(solution)/shard_map/ppermute | solution.py:14
  142.6 20.5 %reduce-scatter.8.cloned.1.call-done = f32[1,8,128]{1,2,0:T(8,128)} async-done(((f32[1,8,512]{1,2,0:T(8,128)}), f32[1,8,128]{1,2,0:T(8,128)}) %reduce-scatter.8.cloned.1.call-update) | async-done | bytes 4112 | tf_op jit(solution)/shard_map/reduce_scatter | solution.py:68
  167.2 4.0 %collective-permute-done.16 = f32[144,128]{1,0:T(8,128)S(1)} collective-permute-done((f32[144,128]{1,0:T(8,128)S(1)}, f32[144,128]{1,0:T(8,128)S(1)}, u32[]{:S(2)}, u32[]{:S(2)}) %collective-permute-start.16) | collective-permute-done | bytes 73760 | tf_op jit(solution)/shard_map/ppermute | solution.py:45
  172.8 2.9 %collective-permute-done.17 = f32[144,128]{1,0:T(8,128)S(1)} collective-permute-done((f32[144,128]{1,0:T(8,128)S(1)}, f32[144,128]{1,0:T(8,128)S(1)}, u32[]{:S(2)}, u32[]{:S(2)}) %collective-permute-start.17) | collective-permute-done | bytes 73760 | tf_op jit(solution)/shard_map/ppermute | solution.py:14
  177.2 2.9 %collective-permute-done.18 = f32[144,128]{1,0:T(8,128)S(1)} collective-permute-done((f32[144,128]{1,0:T(8,128)S(1)}, f32[144,128]{1,0:T(8,128)S(1)}, u32[]{:S(2)}, u32[]{:S(2)}) %collective-permute-start.18) | collective-permute-done | bytes 73760 | tf_op jit(solution)/shard_map/ppermute | solution.py:14
  180.2 3.1 %collective-permute-start.19 = (f32[144,128]{1,0:T(8,128)S(1)}, f32[144,128]{1,0:T(8,128)S(1)}, u32[]{:S(2)}, u32[]{:S(2)}) collective-permute-start(f32[144,128]{1,0:T(8,128)S(1)} %add.260), channel_id=1, source_target_pairs={{0,16},{4,20},{8,24},{12,28},{16,0},{20,4},{24,8},{28,12},{1,17},{... | collective-permute-start | bytes 221192 | tf_op jit(solution)/shard_map/ppermute | solution.py:14
  187.7 3.0 %collective-permute-done.21 = f32[8,128]{1,0:T(8,128)S(1)} collective-permute-done((f32[8,128]{1,0:T(8,128)S(1)}, f32[8,128]{1,0:T(8,128)S(1)}, u32[]{:S(2)}, u32[]{:S(2)}) %collective-permute-start.21) | collective-permute-done | bytes 4128 | tf_op jit(solution)/shard_map/ppermute | solution.py:45
  198.0 3.0 %collective-permute-start.24 = (f32[8,128]{1,0:T(8,128)S(1)}, f32[8,128]{1,0:T(8,128)S(1)}, u32[]{:S(2)}, u32[]{:S(2)}) collective-permute-start(f32[8,128]{1,0:T(8,128)S(1)} %add.266), channel_id=1, source_target_pairs={{0,16},{4,20},{8,24},{12,28},{16,0},{20,4},{24,8},{28,12},{1,17},{... | collective-permute-start | bytes 12296 | tf_op jit(solution)/shard_map/ppermute | solution.py:14
  202.8 5.4 %all-gather = f32[8,512]{1,0:T(8,128)S(1)} all-gather(f32[8,128]{1,0:T(8,128)S(1)} %convolution_add_fusion.3), channel_id=2, replica_groups=mesh['leaf'=8,'grid'=4] {'grid'}, dimensions={1}, use_global_device_ids=true | all-gather | bytes 20480 | tf_op jit(solution)/shard_map/all_gather | solution.py:72
  215.8 3.0 %collective-permute-start.27 = (f32[1,8,2048]{2,1,0:T(8,128)S(1)}, f32[1,8,2048]{2,1,0:T(8,128)S(1)}, u32[]{:S(2)}, u32[]{:S(2)}) collective-permute-start(f32[1,8,2048]{2,1,0:T(8,128)S(1)} %maximum_select_fusion.2), channel_id=1, source_target_pairs={{0,16},{4,20},{8,24},{12,28},{16,0},{20,4},{24,8},{28,12},{1,17},{... | collective-permute-start | bytes 196616 | tf_op jit(solution)/shard_map/ppermute | solution.py:14
  224.4 3.1 %collective-permute-done.29 = f32[16,128]{1,0:T(8,128)S(1)} collective-permute-done((f32[16,128]{1,0:T(8,128)S(1)}, f32[16,128]{1,0:T(8,128)S(1)}, u32[]{:S(2)}, u32[]{:S(2)}) %collective-permute-start.29) | collective-permute-done | bytes 8224 | tf_op jit(solution)/shard_map/ppermute | solution.py:45
  235.7 5.2 %all_gather.10 = f32[2,8,512]{2,1,0:T(8,128)S(1)} all-gather(f32[2,8,128]{2,1,0:T(8,128)S(1)} %pad_maximum_fusion.7), channel_id=1, replica_groups=mesh['leaf'=8,'grid'=4] {'grid'}, dimensions={2}, use_global_device_ids=true | all-gather | bytes 40960 | tf_op jit(solution)/shard_map/all_gather | solution.py:72
  252.7 2.9 %collective-permute-done.35 = f32[16,128]{1,0:T(8,128)S(1)} collective-permute-done((f32[16,128]{1,0:T(8,128)S(1)}, f32[16,128]{1,0:T(8,128)S(1)}, u32[]{:S(2)}, u32[]{:S(2)}) %collective-permute-start.35) | collective-permute-done | bytes 8224 | tf_op jit(solution)/shard_map/ppermute | solution.py:45
  260.1 5.2 %all_gather.11 = f32[2,8,512]{2,1,0:T(8,128)S(1)} all-gather(f32[2,8,128]{2,1,0:T(8,128)S(1)} %pad_maximum_fusion.9), channel_id=1, replica_groups=mesh['leaf'=8,'grid'=4] {'grid'}, dimensions={2}, use_global_device_ids=true | all-gather | bytes 40960 | tf_op jit(solution)/shard_map/all_gather | solution.py:72
  272.5 3.1 %collective-permute-done.39 = f32[16,128]{1,0:T(8,128)S(1)} collective-permute-done((f32[16,128]{1,0:T(8,128)S(1)}, f32[16,128]{1,0:T(8,128)S(1)}, u32[]{:S(2)}, u32[]{:S(2)}) %collective-permute-start.39) | collective-permute-done | bytes 8224 | tf_op jit(solution)/shard_map/ppermute | solution.py:45
  (337 shorter events, 130.0 us)
Async XLA Ops:
  7.2 43.1 %reduce-scatter.4.cloned.1.call-start = ((), (), s32[]{:S(2)}) async-start(), calls=%async_computation.3 | async-start | bytes 40960 | tf_op jit(solution)/shard_map/reduce_scatter | solution.py:68
  11.5 4.3 %collective-permute-start = (f32[144,128]{1,0:T(8,128)S(1)}, f32[144,128]{1,0:T(8,128)S(1)}, u32[]{:S(2)}, u32[]{:S(2)}) collective-permute-start(f32[144,128]{1,0:T(8,128)S(1)} %pad_maximum_fusion), channel_id=1, source_target_pairs={{0,1},{1,0},{2,3},{3,2},{4,5},{5,4},{6,7},{7,6},{8,9},{9,8},{10,11... | collective-permute-start | bytes 221192 | tf_op jit(solution)/shard_map/ppermute | solution.py:45
  15.8 5.5 %collective-permute-start.1 = (f32[144,128]{1,0:T(8,128)S(1)}, f32[144,128]{1,0:T(8,128)S(1)}, u32[]{:S(2)}, u32[]{:S(2)}) collective-permute-start(f32[144,128]{1,0:T(8,128)S(1)} %fusion.129), channel_id=1, source_target_pairs={{0,2},{1,3},{2,0},{3,1},{4,6},{5,7},{6,4},{7,5},{8,10},{9,11},{10,... | collective-permute-start | bytes 221192 | tf_op jit(solution)/shard_map/ppermute | solution.py:45
  24.5 4.0 %collective-permute-start.2 = (f32[2,8,512]{2,1,0:T(8,128)S(1)}, f32[2,8,512]{2,1,0:T(8,128)S(1)}, u32[]{:S(2)}, u32[]{:S(2)}) collective-permute-start(f32[2,8,512]{2,1,0:T(8,128)S(1)} %broadcast_select_fusion.1), channel_id=1, source_target_pairs={{0,4},{4,0},{8,12},{12,8},{16,20},{20,16},{24,28},{28,24},{1,5},{5... | collective-permute-start | bytes 98312 | tf_op jit(solution)/shard_map/ppermute | solution.py:14
  29.1 68.2 %reduce-scatter.6.cloned.1.call-start = ((), (), s32[]{:S(2)}) async-start(), calls=%async_computation.4 | async-start | bytes 40960 | tf_op jit(solution)/shard_map/reduce_scatter | solution.py:68
  53.5 4.4 %collective-permute-start.4 = (f32[144,128]{1,0:T(8,128)S(1)}, f32[144,128]{1,0:T(8,128)S(1)}, u32[]{:S(2)}, u32[]{:S(2)}) collective-permute-start(f32[144,128]{1,0:T(8,128)S(1)} %fusion.128), channel_id=1, source_target_pairs={{0,2},{1,3},{2,0},{3,1},{4,6},{5,7},{6,4},{7,5},{8,10},{9,11},{10,... | collective-permute-start | bytes 221192 | tf_op jit(solution)/shard_map/ppermute | solution.py:45
  57.9 4.4 %collective-permute-start.5 = (f32[144,128]{1,0:T(8,128)S(1)}, f32[144,128]{1,0:T(8,128)S(1)}, u32[]{:S(2)}, u32[]{:S(2)}) collective-permute-start(f32[144,128]{1,0:T(8,128)S(1)} %add.232), channel_id=1, source_target_pairs={{0,4},{4,0},{8,12},{12,8},{16,20},{20,16},{24,28},{28,24},{1,5},{5... | collective-permute-start | bytes 221192 | tf_op jit(solution)/shard_map/ppermute | solution.py:14
  68.7 4.3 %collective-permute-start.6 = (f32[2,8,1024]{2,1,0:T(8,128)S(1)}, f32[2,8,1024]{2,1,0:T(8,128)S(1)}, u32[]{:S(2)}, u32[]{:S(2)}) collective-permute-start(f32[2,8,1024]{2,1,0:T(8,128)S(1)} %broadcast_select_fusion), channel_id=1, source_target_pairs={{0,8},{4,12},{8,0},{12,4},{16,24},{20,28},{24,16},{28,20},{1,9},{5... | collective-permute-start | bytes 196616 | tf_op jit(solution)/shard_map/ppermute | solution.py:14
  73.1 4.0 %collective-permute-start.7 = (f32[2,8,512]{2,1,0:T(8,128)S(1)}, f32[2,8,512]{2,1,0:T(8,128)S(1)}, u32[]{:S(2)}, u32[]{:S(2)}) collective-permute-start(f32[2,8,512]{2,1,0:T(8,128)S(1)} %slice_select_fusion.3), channel_id=1, source_target_pairs={{0,4},{4,0},{8,12},{12,8},{16,20},{20,16},{24,28},{28,24},{1,5},{5... | collective-permute-start | bytes 98312 | tf_op jit(solution)/shard_map/ppermute | solution.py:14
  77.7 85.3 %reduce-scatter.8.cloned.1.call-start = ((), (), s32[]{:S(2)}) async-start(), calls=%async_computation.5 | async-start | bytes 327680 | tf_op jit(solution)/shard_map/reduce_scatter | solution.py:68
  100.6 4.4 %collective-permute-start.9 = (f32[144,128]{1,0:T(8,128)S(1)}, f32[144,128]{1,0:T(8,128)S(1)}, u32[]{:S(2)}, u32[]{:S(2)}) collective-permute-start(f32[144,128]{1,0:T(8,128)S(1)} %fusion.127), channel_id=1, source_target_pairs={{0,2},{1,3},{2,0},{3,1},{4,6},{5,7},{6,4},{7,5},{8,10},{9,11},{10,... | collective-permute-start | bytes 221192 | tf_op jit(solution)/shard_map/ppermute | solution.py:45
  105.0 4.4 %collective-permute-start.10 = (f32[144,128]{1,0:T(8,128)S(1)}, f32[144,128]{1,0:T(8,128)S(1)}, u32[]{:S(2)}, u32[]{:S(2)}) collective-permute-start(f32[144,128]{1,0:T(8,128)S(1)} %add.244), channel_id=1, source_target_pairs={{0,4},{4,0},{8,12},{12,8},{16,20},{20,16},{24,28},{28,24},{1,5},{5... | collective-permute-start | bytes 221192 | tf_op jit(solution)/shard_map/ppermute | solution.py:14
  109.4 4.4 %collective-permute-start.11 = (f32[144,128]{1,0:T(8,128)S(1)}, f32[144,128]{1,0:T(8,128)S(1)}, u32[]{:S(2)}, u32[]{:S(2)}) collective-permute-start(f32[144,128]{1,0:T(8,128)S(1)} %add.245), channel_id=1, source_target_pairs={{0,8},{4,12},{8,0},{12,4},{16,24},{20,28},{24,16},{28,20},{1,9},{5... | collective-permute-start | bytes 221192 | tf_op jit(solution)/shard_map/ppermute | solution.py:14
  118.1 5.5 %collective-permute-start.12 = (f32[1,8,2048]{2,1,0:T(8,128)}, f32[1,8,2048]{2,1,0:T(8,128)}, u32[]{:S(2)}, u32[]{:S(2)}) collective-permute-start(f32[1,8,2048]{2,1,0:T(8,128)} %copy.65), channel_id=1, source_target_pairs={{0,16},{4,20},{8,24},{12,28},{16,0},{20,4},{24,8},{28,12},{1,17},{... | collective-permute-start | bytes 196616 | tf_op jit(solution)/shard_map/ppermute | solution.py:14
  125.0 9.7 %collective-permute-start.13 = (f32[1,8,1024]{1,2,0:T(8,128)S(1)}, f32[1,8,1024]{1,2,0:T(8,128)S(1)}, u32[]{:S(2)}, u32[]{:S(2)}) collective-permute-start(f32[1,8,1024]{1,2,0:T(8,128)S(1)} %slice_select_fusion.1), channel_id=1, source_target_pairs={{0,8},{4,12},{8,0},{12,4},{16,24},{20,28},{24,16},{28,20},{1,9},{5... | collective-permute-start | bytes 98312 | tf_op jit(solution)/shard_map/ppermute | solution.py:14
  134.9 6.4 %collective-permute-start.14 = (f32[1,8,512]{1,2,0:T(8,128)S(1)}, f32[1,8,512]{1,2,0:T(8,128)S(1)}, u32[]{:S(2)}, u32[]{:S(2)}) collective-permute-start(f32[1,8,512]{1,2,0:T(8,128)S(1)} %slice_select_fusion.2), channel_id=1, source_target_pairs={{0,4},{4,0},{8,12},{12,8},{16,20},{20,16},{24,28},{28,24},{1,5},{5... | collective-permute-start | bytes 49160 | tf_op jit(solution)/shard_map/ppermute | solution.py:14
  166.8 4.4 %collective-permute-start.16 = (f32[144,128]{1,0:T(8,128)S(1)}, f32[144,128]{1,0:T(8,128)S(1)}, u32[]{:S(2)}, u32[]{:S(2)}) collective-permute-start(f32[144,128]{1,0:T(8,128)S(1)} %fusion.126), channel_id=1, source_target_pairs={{0,2},{1,3},{2,0},{3,1},{4,6},{5,7},{6,4},{7,5},{8,10},{9,11},{10,... | collective-permute-start | bytes 221192 | tf_op jit(solution)/shard_map/ppermute | solution.py:45
  171.2 4.4 %collective-permute-start.17 = (f32[144,128]{1,0:T(8,128)S(1)}, f32[144,128]{1,0:T(8,128)S(1)}, u32[]{:S(2)}, u32[]{:S(2)}) collective-permute-start(f32[144,128]{1,0:T(8,128)S(1)} %add.258), channel_id=1, source_target_pairs={{0,4},{4,0},{8,12},{12,8},{16,20},{20,16},{24,28},{28,24},{1,5},{5... | collective-permute-start | bytes 221192 | tf_op jit(solution)/shard_map/ppermute | solution.py:14
  175.7 4.4 %collective-permute-start.18 = (f32[144,128]{1,0:T(8,128)S(1)}, f32[144,128]{1,0:T(8,128)S(1)}, u32[]{:S(2)}, u32[]{:S(2)}) collective-permute-start(f32[144,128]{1,0:T(8,128)S(1)} %add.259), channel_id=1, source_target_pairs={{0,8},{4,12},{8,0},{12,4},{16,24},{20,28},{24,16},{28,20},{1,9},{5... | collective-permute-start | bytes 221192 | tf_op jit(solution)/shard_map/ppermute | solution.py:14
  180.2 5.4 %collective-permute-start.19 = (f32[144,128]{1,0:T(8,128)S(1)}, f32[144,128]{1,0:T(8,128)S(1)}, u32[]{:S(2)}, u32[]{:S(2)}) collective-permute-start(f32[144,128]{1,0:T(8,128)S(1)} %add.260), channel_id=1, source_target_pairs={{0,16},{4,20},{8,24},{12,28},{16,0},{20,4},{24,8},{28,12},{1,17},{... | collective-permute-start | bytes 221192 | tf_op jit(solution)/shard_map/ppermute | solution.py:14
  198.0 4.6 %collective-permute-start.24 = (f32[8,128]{1,0:T(8,128)S(1)}, f32[8,128]{1,0:T(8,128)S(1)}, u32[]{:S(2)}, u32[]{:S(2)}) collective-permute-start(f32[8,128]{1,0:T(8,128)S(1)} %add.266), channel_id=1, source_target_pairs={{0,16},{4,20},{8,24},{12,28},{16,0},{20,4},{24,8},{28,12},{1,17},{... | collective-permute-start | bytes 12296 | tf_op jit(solution)/shard_map/ppermute | solution.py:14
  211.9 3.9 %collective-permute-start.26 = (f32[1,8,1024]{2,1,0:T(8,128)S(1)}, f32[1,8,1024]{2,1,0:T(8,128)S(1)}, u32[]{:S(2)}, u32[]{:S(2)}) collective-permute-start(f32[1,8,1024]{2,1,0:T(8,128)S(1)} %maximum_select_fusion.6), channel_id=1, source_target_pairs={{0,8},{4,12},{8,0},{12,4},{16,24},{20,28},{24,16},{28,20},{1,9},{5... | collective-permute-start | bytes 98312 | tf_op jit(solution)/shard_map/ppermute | solution.py:14
  215.8 5.2 %collective-permute-start.27 = (f32[1,8,2048]{2,1,0:T(8,128)S(1)}, f32[1,8,2048]{2,1,0:T(8,128)S(1)}, u32[]{:S(2)}, u32[]{:S(2)}) collective-permute-start(f32[1,8,2048]{2,1,0:T(8,128)S(1)} %maximum_select_fusion.2), channel_id=1, source_target_pairs={{0,16},{4,20},{8,24},{12,28},{16,0},{20,4},{24,8},{28,12},{1,17},{... | collective-permute-start | bytes 196616 | tf_op jit(solution)/shard_map/ppermute | solution.py:14
  244.8 4.3 %collective-permute-start.33 = (f32[2,8,1024]{2,1,0:T(8,128)S(1)}, f32[2,8,1024]{2,1,0:T(8,128)S(1)}, u32[]{:S(2)}, u32[]{:S(2)}) collective-permute-start(f32[2,8,1024]{2,1,0:T(8,128)S(1)} %maximum_select_fusion.4), channel_id=1, source_target_pairs={{0,8},{4,12},{8,0},{12,4},{16,24},{20,28},{24,16},{28,20},{1,9},{5... | collective-permute-start | bytes 196616 | tf_op jit(solution)/shard_map/ppermute | solution.py:14
  (79 other events, 2036.5 us)
Sparse Core Ops, SparseCore 0:
  29.2 20.9 reduce-scatter.3
  77.8 19.5 reduce-scatter.5
  142.3 20.7 reduce-scatter.7
